TPU v7x, 32 devices: a whole 2x2x4 slice. The times are simulated.
32 devices in a mesh: field: 2 (over x), ep: 16 (over z, y, core).
Axes of the slice: x: 2, y: 2, z: 4, core: 2. Of those that a mesh axis runs over, the one named last changes fastest.
Arguments:
- images: float32 [64, 16, 256], P(('field', 'ep')), parts along dimension 0, may hold values from -6 to 6
- reference_image: float32 [32, 256], P('field'), parts along dimension 0, may hold values from -6 to 6
- kernels: float32 [16, 23, 23], replicated, may hold values from -0.25 to 0.25
- kernel_index: int32 [64], P(('field', 'ep')), parts along dimension 0, may hold values from 0 to 15
- tile_mask: int32 [64, 16, 2], P(('field', 'ep')), parts along dimension 0, may hold values 0 or 1
- systematics: float32 [64, 40], P('field'), parts along dimension 0, may hold values from -6 to 6
- onsets: int32 [16], P('field'), parts along dimension 0, may hold values from 0 to 27
Outputs:
- coefficients: float32 [48, 32, 256], P(None, ('field', 'ep')), parts along dimension 1
- epoch_scatter: float32 [64], P('field'), parts along dimension 0
There are 2 independent parts, one for each index of `field`. A program takes and returns all parts, laid end to end along the dimension named above; an argument that names none is the same for every part. Nothing has to cross between parts.
All inputs are finite; a program needn't handle non-finite values. No bound on the sum of `tile_mask` on one device may be relied on, other than what follows from the above.
Results may differ from a plain program's by a relative error of at most 0.00011.
Values sent between devices are 32-bit elements; how exact they have to be, the bound alone decides.
A program may use at most 64 MiB of HBM per device.

v0:
```python
import math
import jax
import jax.numpy as jnp
from jax import lax
from jax.sharding import PartitionSpec as P

cov_ridge = 0.5
fit_ridge = 1.0


def correlate(stack, chosen):
    count, rows, width = stack.shape
    side = chosen.shape[1]
    half = (side - 1) // 2
    padded = jnp.pad(stack, ((0, 0), (half, half), (half, half)))
    filters = jnp.transpose(chosen, (1, 2, 0))[:, :, None, :]
    strip = math.gcd(rows, 16)

    def one_strip(start):
        piece = lax.dynamic_slice_in_dim(padded, start, strip + 2 * half, 1)
        result = lax.conv_general_dilated(
            piece[None],
            filters,
            (1, 1),
            "VALID",
            dimension_numbers=("NCHW", "HWIO", "NCHW"),
            feature_group_count=count,
            precision=lax.Precision.HIGHEST,
        )
        return result[0]

    starts = jnp.arange(rows // strip, dtype=jnp.int32) * strip
    strips = lax.map(one_strip, starts)
    return jnp.transpose(strips, (1, 0, 2, 3)).reshape(count, rows, width)


def subtract(stack, reference_image, chosen, masks):
    result = reference_image[None] - correlate(stack, chosen)
    shape = result.shape
    tiles = result.reshape(shape[0], shape[1], shape[2] // 128, 128) * masks[..., None].astype(
        jnp.float32
    )
    return tiles.reshape(shape)


def build_design(systematics, onsets):
    count = systematics.shape[0]
    templates = onsets.shape[0]
    epoch_axis = jnp.arange(count, dtype=jnp.float32)[:, None]
    delays = epoch_axis - onsets[None, :].astype(jnp.float32)
    timescale = (jnp.arange(templates, dtype=jnp.float32) + 1.0) * count / (2.0 * templates)
    transient = jnp.where(
        delays >= 0.0, jnp.exp(-jnp.maximum(delays, 0.0) / timescale[None, :]), 0.0
    )
    return jnp.concatenate([systematics, transient], axis=1)


def fit_matrix(scatter, npixels, design):
    count = design.shape[0]
    columns = design.shape[1]
    covariance = scatter / npixels + cov_ridge * jnp.eye(count, dtype=scatter.dtype)
    lower = jnp.linalg.cholesky(covariance)
    weighted = jax.scipy.linalg.cho_solve((lower, True), design)
    normal = jnp.dot(design.T, weighted, precision=lax.Precision.HIGHEST) + fit_ridge * jnp.eye(
        columns, dtype=scatter.dtype
    )
    lower_fit = jnp.linalg.cholesky(normal)
    return jax.scipy.linalg.cho_solve((lower_fit, True), weighted.T)


def shards(images, reference_image, kernels, kernel_index, tile_mask, systematics, onsets):
    local_count, rows, width = images.shape
    basis = kernels.shape[0]
    side = kernels.shape[1]
    onehot = (kernel_index[:, None] == jnp.arange(basis, dtype=jnp.int32)[None, :]).astype(
        jnp.float32
    )
    chosen = jnp.dot(
        onehot, kernels.reshape(basis, side * side), precision=lax.Precision.HIGHEST
    ).reshape(local_count, side, side)
    difference = subtract(images, reference_image, chosen, tile_mask)
    received = lax.all_to_all(difference, "ep", split_axis=1, concat_axis=0, tiled=True)
    count = received.shape[0]
    block_rows = received.shape[1]
    pixel_data = received.reshape(count, block_rows * width)
    partial_value = jnp.dot(pixel_data, pixel_data.T, precision=lax.Precision.HIGHEST)
    scatter = lax.psum(partial_value, "ep")
    npixels = float(rows * width)
    design = build_design(systematics, onsets)
    fit = fit_matrix(scatter, npixels, design)
    coefficients = jnp.dot(fit, pixel_data, precision=lax.Precision.HIGHEST)
    projector = jnp.eye(count, dtype=jnp.float32) - jnp.dot(
        design, fit, precision=lax.Precision.HIGHEST
    )
    product = jnp.dot(projector, scatter, precision=lax.Precision.HIGHEST)
    epoch_scatter = jnp.sum(product * projector, axis=1) / npixels
    return (coefficients.reshape(design.shape[1], block_rows, width), epoch_scatter)


def solution(mesh):
    in_specs = (
        P(("field", "ep"), None, None),
        P("field", None),
        P(),
        P(("field", "ep")),
        P(("field", "ep"), None, None),
        P("field", None),
        P("field"),
    )
    out_specs = (P(None, ("field", "ep"), None), P("field"))
    return jax.shard_map(shards, mesh=mesh, in_specs=in_specs, out_specs=out_specs, check_vma=False)
```

profile of v0, /device:TPU:0, one launch (start us, length us, event | category | flops | bytes accessed | tf_op | source)
XLA Modules:
  0.0 186.9 jit_solution(5411633704186777744)
XLA Ops:
  0.6 0.8 pad_bitcast_fusion
  1.5 0.0 copy-start
  1.5 0.0 copy-start.5
  1.5 0.0 copy-start.4
  1.5 7.8 %copy.30 = f32[1,2,38,278]{1,0,3,2:T(1,128)} copy(f32[1,2,38,278]{3,2,1,0:T(8,128)S(1)} %pad_bitcast_fusion) | data formatting | bytes 169024 | tf_op jit(solution)/shard_map/while/body/eval_jaxpr/broadcast_in_dim | solution.py:22
  9.3 0.0 copy-done
  9.3 0.1 copy.28
  9.3 0.1 reshape.61
  9.5 0.1 dot_general.25
  9.6 0.0 copy-done.5
  9.6 0.2 convolution_bitcast_fusion.1
  9.8 0.3 copy.31
  10.1 0.0 copy-done.4
  10.1 0.7 copy.32
  10.8 0.0 copy-start.2
  10.8 0.0 copy-start.3
  10.8 82.8 %fusion.21 = f32[1,2,16,256]{1,0,3,2:T(1,128)S(1)} fusion(f32[1,2,38,278]{1,0,3,2:T(1,128)} %copy.30, f32[23,23,1,2]{3,2,1,0:T(1,128)S(1)} %copy.31), kind=kOutput, calls=%fused_computation.46 | convolution fusion | flops 52002816 | bytes 121512 | tf_op jit(solution)/shard_map/while/body/eval_jaxpr/conv_general_dilated | solution.py:21
  93.6 0.0 copy-done.2
  93.6 0.0 copy-done.3
  93.6 0.9 bitcast_multiply_fusion
  94.5 0.0 copy-start.6
  94.5 0.0 copy-start.1
  94.5 1.2 copy.33
  95.8 7.4 %all-to-all-start = ((f32[2,16,256]{2,0,1:T(2,128)}), f32[2,16,256]{2,0,1:T(2,128)S(1)}, u32[]{:S(2)}, u32[]{:S(2)}) async-start(f32[2,16,256]{2,0,1:T(2,128)} %copy.33), calls=%async_computation | async-start | bytes 65536 | tf_op jit(solution)/shard_map/all_to_all | solution.py:82
  103.2 0.0 copy-done.6
  103.2 6.6 %all-to-all-done = f32[2,16,256]{2,0,1:T(2,128)S(1)} async-done(((f32[2,16,256]{2,0,1:T(2,128)}), f32[2,16,256]{2,0,1:T(2,128)S(1)}, u32[]{:S(2)}, u32[]{:S(2)}) %all-to-all-start) | async-done | bytes 32800 | tf_op jit(solution)/shard_map/all_to_all | solution.py:82
  109.8 0.2 fusion.22
  110.0 57.7 %psum.7 = f32[32,32]{1,0:T(8,128)S(1)} all-reduce(f32[32,32]{1,0:T(8,128)S(1)} %fusion.22), channel_id=1, replica_groups=mesh['field'=2,'ep'=16] {'ep'}, use_global_device_ids=true, to_apply=%region_0.1 | all-reduce | flops 1024 | bytes 8192 | tf_op jit(solution)/shard_map/psum | solution.py:87
  167.7 0.1 copy.34
  167.8 2.9 %cholesky.34 = f32[32,32]{1,0:T(8,128)S(1)} custom-call(f32[32,32]{1,0:T(8,128)S(1)} %fusion.14), custom_call_target="Cholesky" | custom-call | tf_op jit(solution)/shard_map/jit(cholesky)/cholesky | solution.py:62
  170.7 0.6 compare_reduce_fusion.1
  171.4 0.7 fusion.9
  172.0 2.4 %custom-call.20 = f32[1,32,32]{1,2,0:T(8,128)S(1)} custom-call(f32[1,32,32]{2,1,0:T(8,128)S(1)} %fusion.9), custom_call_target="InvertDiagBlocksLowerTriangular" | custom-call | tf_op jit(solution)/shard_map/jit(_cho_solve)/triangular_solve | solution.py:63
  174.4 0.0 copy-done.1
  174.4 0.3 fusion.12
  174.7 0.1 fusion.10
  174.8 0.3 fusion.20
  175.2 0.1 copy.35
  175.3 4.4 %cholesky.64 = f32[48,48]{1,0:T(8,128)S(1)} custom-call(f32[48,48]{1,0:T(8,128)S(1)} %fusion.8), custom_call_target="Cholesky" | custom-call | tf_op jit(solution)/shard_map/jit(cholesky)/cholesky | solution.py:67
  179.7 0.6 compare_reduce_fusion
  180.3 0.7 fusion.2
  181.0 3.7 %custom-call.21 = f32[1,48,48]{1,2,0:T(8,128)S(1)} custom-call(f32[1,48,48]{2,1,0:T(8,128)S(1)} %fusion.2), custom_call_target="InvertDiagBlocksLowerTriangular" | custom-call | tf_op jit(solution)/shard_map/jit(_cho_solve)/triangular_solve | solution.py:68
  184.7 0.2 fusion.5
  184.8 0.2 fusion.3
  185.0 0.2 convolution_subtract_fusion
  185.2 0.2 convolution_bitcast_fusion
  185.5 0.2 fusion
  185.7 0.5 broadcast_multiply_fusion
  186.2 0.7 copy.38
  (10 shorter events, 0.2 us)
Async XLA Ops:
  1.5 7.8 %copy-start = (f32[16,23,23]{2,0,1:T(8,128)S(1)}, f32[16,23,23]{2,0,1:T(8,128)}, u32[]{:S(2)}) copy-start(f32[16,23,23]{2,0,1:T(8,128)} %param.9) | copy-start | bytes 101572
  1.5 8.1 %copy-start.5 = (s32[2]{0:T(128)S(1)}, s32[2]{0:T(128)}, u32[]{:S(2)}) copy-start(s32[2]{0:T(128)} %param.10) | copy-start | bytes 28
  1.5 8.6 %copy-start.4 = (s32[2,16,2]{1,2,0:T(2,128)S(1)}, s32[2,16,2]{1,2,0:T(2,128)}, u32[]{:S(2)}) copy-start(s32[2,16,2]{1,2,0:T(2,128)} %param.11) | copy-start | bytes 772
  10.8 82.8 %copy-start.2 = (f32[2,16,2]{0,2,1:T(2,128)S(1)}, f32[2,16,2]{0,2,1:T(2,128)}, u32[]{:S(2)}) copy-start(f32[2,16,2]{0,2,1:T(2,128)} %copy.32) | copy-start | bytes 772
  10.8 82.8 %copy-start.3 = (f32[16,256]{1,0:T(8,128)S(1)}, f32[16,256]{1,0:T(8,128)}, u32[]{:S(2)}) copy-start(f32[16,256]{1,0:T(8,128)} %param.8) | copy-start | bytes 49156
  94.5 8.7 %copy-start.6 = (s32[8]{0:T(128)S(1)}, s32[8]{0:T(128)}, u32[]{:S(2)}) copy-start(s32[8]{0:T(128)} %param.13) | copy-start | bytes 100
  94.5 79.9 %copy-start.1 = (f32[32,40]{1,0:T(8,128)S(1)}, f32[32,40]{1,0:T(8,128)}, u32[]{:S(2)}) copy-start(f32[32,40]{1,0:T(8,128)} %param.12) | copy-start | bytes 15364
  95.8 14.1 %all-to-all-start = ((f32[2,16,256]{2,0,1:T(2,128)}), f32[2,16,256]{2,0,1:T(2,128)S(1)}, u32[]{:S(2)}, u32[]{:S(2)}) async-start(f32[2,16,256]{2,0,1:T(2,128)} %copy.33), calls=%async_computation | async-start | bytes 65536 | tf_op jit(solution)/shard_map/all_to_all | solution.py:82
where the time goes:
time: 187 us
  matrix products  84.9 us (45%)
  blocking collectives  57.7 us (31%)
  other arithmetic  17.5 us (9%)
  local copies, waits for them, and re-layouts  12 us (6%)
  starting transfers between devices  7.41 us (4%)
  waiting for transfers between devices  6.57 us (4%)
    conv_general_dilated x1, matrix products, one_strip(): lax.conv_general_dilated(piece[None], filters, (1, 1), 'VALID', dimension...  82.8 us
    psum x1, blocking collectives, shards(): scatter = lax.psum(partial_value, 'ep')  57.7 us
    broadcast_in_dim x2, local copies, waits for them, and re-layouts, one_strip(): piece[None]  8.6 us
    all_to_all x1, starting transfers between devices, shards(): lax.all_to_all(difference, 'ep', split_axis=1, concat_axis=0, tiled=True)  7.41 us
    all_to_all x1, waiting for transfers between devices, shards(): lax.all_to_all(difference, 'ep', split_axis=1, concat_axis=0, tiled=True)  6.57 us
    another operation x3, other arithmetic, fit_matrix(): lower_fit = jnp.linalg.cholesky(normal)  5.05 us
    another operation x2, other arithmetic, fit_matrix(): return jax.scipy.linalg.cho_solve((lower_fit, True), weighted.T)  4.32 us
  transfers between devices with their start and end apart: 1, of which 1 were waited for; matrix products, arithmetic and copies ran while one was open for 0% of the time, Pallas kernels for 0%

commit v1 on v0

--- a/solution.py
+++ b/solution.py
@@ -3,6 +3,7 @@
 import jax.numpy as jnp
 from jax import lax
 from jax.sharding import PartitionSpec as P
+from jax.lax import all_gather
 
 cov_ridge = 0.5
 fit_ridge = 1.0
@@ -84,7 +85,7 @@
     block_rows = received.shape[1]
     pixel_data = received.reshape(count, block_rows * width)
     partial_value = jnp.dot(pixel_data, pixel_data.T, precision=lax.Precision.HIGHEST)
-    scatter = lax.psum(partial_value, "ep")
+    scatter = jnp.sum(all_gather(partial_value, axis_name="ep"), 0)
     npixels = float(rows * width)
     design = build_design(systematics, onsets)
     fit = fit_matrix(scatter, npixels, design)

time: 187 us -> 148 us (0.79)
  blocking collectives: 57.7 us -> 18.3 us
    psum x1 -> x0, blocking collectives: 57.7 us -> none  [shards(): scatter = lax.psum(partial_value, 'ep')]
    all_gather x0 -> x1, blocking collectives: none -> 18.3 us  [shards(): scatter = jnp.sum(all_gather(partial_value, axis_name='ep'), 0)]
where the time goes in v1:
time: 148 us
  matrix products  84.9 us (57%)
  blocking collectives  18.3 us (12%)
  other arithmetic  17.6 us (12%)
  local copies, waits for them, and re-layouts  12.1 us (8%)
  starting transfers between devices  7.41 us (5%)
  waiting for transfers between devices  6.57 us (4%)
    conv_general_dilated x1, matrix products, one_strip(): lax.conv_general_dilated(piece[None], filters, (1, 1), 'VALID', dimension...  82.8 us
    all_gather x1, blocking collectives, shards(): scatter = jnp.sum(all_gather(partial_value, axis_name='ep'), 0)  18.3 us
    broadcast_in_dim x2, local copies, waits for them, and re-layouts, one_strip(): piece[None]  8.6 us
    all_to_all x1, starting transfers between devices, shards(): lax.all_to_all(difference, 'ep', split_axis=1, concat_axis=0, tiled=True)  7.41 us
    all_to_all x1, waiting for transfers between devices, shards(): lax.all_to_all(difference, 'ep', split_axis=1, concat_axis=0, tiled=True)  6.57 us
    another operation x3, other arithmetic, fit_matrix(): lower_fit = jnp.linalg.cholesky(normal)  5.05 us
    another operation x2, other arithmetic, fit_matrix(): return jax.scipy.linalg.cho_solve((lower_fit, True), weighted.T)  4.32 us
    another operation x3, other arithmetic, fit_matrix(): lower = jnp.linalg.cholesky(covariance)  3.59 us
  transfers between devices with their start and end apart: 1, of which 1 were waited for; matrix products, arithmetic and copies ran while one was open for 0% of the time, Pallas kernels for 0%

profile of v1, /device:TPU:0, one launch (start us, length us, event | category | flops | bytes accessed | tf_op | source)
XLA Modules:
  0.0 147.6 jit_solution(16331697867244578750)
XLA Ops:
  0.6 0.8 pad_bitcast_fusion
  1.5 0.0 copy-start
  1.5 0.0 copy-start.5
  1.5 0.0 copy-start.4
  1.5 7.8 %copy.30 = f32[1,2,38,278]{1,0,3,2:T(1,128)} copy(f32[1,2,38,278]{3,2,1,0:T(8,128)S(1)} %pad_bitcast_fusion) | data formatting | bytes 169024 | tf_op jit(solution)/shard_map/while/body/eval_jaxpr/broadcast_in_dim | solution.py:23
  9.3 0.0 copy-done
  9.3 0.1 copy.28
  9.3 0.1 reshape.61
  9.5 0.1 dot_general.25
  9.6 0.0 copy-done.5
  9.6 0.2 convolution_bitcast_fusion.1
  9.8 0.3 copy.31
  10.1 0.0 copy-done.4
  10.1 0.7 copy.32
  10.8 0.0 copy-start.2
  10.8 0.0 copy-start.3
  10.8 82.8 %fusion.22 = f32[1,2,16,256]{1,0,3,2:T(1,128)S(1)} fusion(f32[1,2,38,278]{1,0,3,2:T(1,128)} %copy.30, f32[23,23,1,2]{3,2,1,0:T(1,128)S(1)} %copy.31), kind=kOutput, calls=%fused_computation.48 | convolution fusion | flops 52002816 | bytes 121512 | tf_op jit(solution)/shard_map/while/body/eval_jaxpr/conv_general_dilated | solution.py:22
  93.6 0.0 copy-done.2
  93.6 0.0 copy-done.3
  93.6 0.9 bitcast_multiply_fusion
  94.5 0.0 copy-start.6
  94.5 0.0 copy-start.1
  94.5 1.2 copy.33
  95.8 7.4 %all-to-all-start = ((f32[2,16,256]{2,0,1:T(2,128)}), f32[2,16,256]{2,0,1:T(2,128)S(1)}, u32[]{:S(2)}, u32[]{:S(2)}) async-start(f32[2,16,256]{2,0,1:T(2,128)} %copy.33), calls=%async_computation | async-start | bytes 65536 | tf_op jit(solution)/shard_map/all_to_all | solution.py:83
  103.2 0.0 copy-done.6
  103.2 6.6 %all-to-all-done = f32[2,16,256]{2,0,1:T(2,128)S(1)} async-done(((f32[2,16,256]{2,0,1:T(2,128)}), f32[2,16,256]{2,0,1:T(2,128)S(1)}, u32[]{:S(2)}, u32[]{:S(2)}) %all-to-all-start) | async-done | bytes 32800 | tf_op jit(solution)/shard_map/all_to_all | solution.py:83
  109.8 0.2 fusion.23
  110.0 18.3 %all-gather = f32[512,32]{1,0:T(8,128)S(1)} all-gather(f32[32,32]{1,0:T(8,128)S(1)} %fusion.23), channel_id=2, replica_groups=mesh['field'=2,'ep'=16] {'ep'}, dimensions={0}, use_global_device_ids=true | all-gather | bytes 69632 | tf_op jit(solution)/shard_map/all_gather | solution.py:88
  128.3 0.1 copy.34
  128.4 0.1 copy.35
  128.5 2.9 %cholesky.34 = f32[32,32]{1,0:T(8,128)S(1)} custom-call(f32[32,32]{1,0:T(8,128)S(1)} %fusion.15), custom_call_target="Cholesky" | custom-call | tf_op jit(solution)/shard_map/jit(cholesky)/cholesky | solution.py:63
  131.4 0.6 compare_reduce_fusion.1
  132.1 0.7 fusion.9
  132.7 2.4 %custom-call.20 = f32[1,32,32]{1,2,0:T(8,128)S(1)} custom-call(f32[1,32,32]{2,1,0:T(8,128)S(1)} %fusion.9), custom_call_target="InvertDiagBlocksLowerTriangular" | custom-call | tf_op jit(solution)/shard_map/jit(_cho_solve)/triangular_solve | solution.py:64
  135.2 0.0 copy-done.1
  135.2 0.3 fusion.12
  135.4 0.1 fusion.10
  135.6 0.3 fusion.21
  135.9 0.1 copy.36
  136.0 4.4 %cholesky.64 = f32[48,48]{1,0:T(8,128)S(1)} custom-call(f32[48,48]{1,0:T(8,128)S(1)} %fusion.8), custom_call_target="Cholesky" | custom-call | tf_op jit(solution)/shard_map/jit(cholesky)/cholesky | solution.py:68
  140.4 0.6 compare_reduce_fusion
  141.0 0.7 fusion.2
  141.7 3.7 %custom-call.21 = f32[1,48,48]{1,2,0:T(8,128)S(1)} custom-call(f32[1,48,48]{2,1,0:T(8,128)S(1)} %fusion.2), custom_call_target="InvertDiagBlocksLowerTriangular" | custom-call | tf_op jit(solution)/shard_map/jit(_cho_solve)/triangular_solve | solution.py:69
  145.4 0.2 fusion.5
  145.5 0.2 fusion.3
  145.7 0.2 convolution_subtract_fusion
  145.9 0.2 convolution_bitcast_fusion
  146.2 0.2 fusion
  146.4 0.5 broadcast_multiply_fusion.1
  146.9 0.7 copy.39
  (11 shorter events, 0.2 us)
Async XLA Ops:
  1.5 7.8 %copy-start = (f32[16,23,23]{2,0,1:T(8,128)S(1)}, f32[16,23,23]{2,0,1:T(8,128)}, u32[]{:S(2)}) copy-start(f32[16,23,23]{2,0,1:T(8,128)} %param.9) | copy-start | bytes 101572
  1.5 8.1 %copy-start.5 = (s32[2]{0:T(128)S(1)}, s32[2]{0:T(128)}, u32[]{:S(2)}) copy-start(s32[2]{0:T(128)} %param.10) | copy-start | bytes 28
  1.5 8.6 %copy-start.4 = (s32[2,16,2]{1,2,0:T(2,128)S(1)}, s32[2,16,2]{1,2,0:T(2,128)}, u32[]{:S(2)}) copy-start(s32[2,16,2]{1,2,0:T(2,128)} %param.11) | copy-start | bytes 772
  10.8 82.8 %copy-start.2 = (f32[2,16,2]{0,2,1:T(2,128)S(1)}, f32[2,16,2]{0,2,1:T(2,128)}, u32[]{:S(2)}) copy-start(f32[2,16,2]{0,2,1:T(2,128)} %copy.32) | copy-start | bytes 772
  10.8 82.8 %copy-start.3 = (f32[16,256]{1,0:T(8,128)S(1)}, f32[16,256]{1,0:T(8,128)}, u32[]{:S(2)}) copy-start(f32[16,256]{1,0:T(8,128)} %param.8) | copy-start | bytes 49156
  94.5 8.7 %copy-start.6 = (s32[8]{0:T(128)S(1)}, s32[8]{0:T(128)}, u32[]{:S(2)}) copy-start(s32[8]{0:T(128)} %param.13) | copy-start | bytes 100
  94.5 40.6 %copy-start.1 = (f32[32,40]{1,0:T(8,128)S(1)}, f32[32,40]{1,0:T(8,128)}, u32[]{:S(2)}) copy-start(f32[32,40]{1,0:T(8,128)} %param.12) | copy-start | bytes 15364
  95.8 14.1 %all-to-all-start = ((f32[2,16,256]{2,0,1:T(2,128)}), f32[2,16,256]{2,0,1:T(2,128)S(1)}, u32[]{:S(2)}, u32[]{:S(2)}) async-start(f32[2,16,256]{2,0,1:T(2,128)} %copy.33), calls=%async_computation | async-start | bytes 65536 | tf_op jit(solution)/shard_map/all_to_all | solution.py:83
